TPU v7x, 32 devices: a whole 2x2x4 slice. The times are simulated.
32 devices in a mesh: terms: 2 (over x), rows: 4 (over y, core), cols: 4 (over z).
Axes of the slice: x: 2, y: 2, z: 4, core: 2. Of those that a mesh axis runs over, the one named last changes fastest.
Arguments:
- wavefunction: bfloat16 [2, 1024, 1024], P(None, 'rows', 'cols'), may hold values from -6 to 6
- energy: float32 [2], replicated, may hold values from 1 to 4
- block_rows: int32 [2], replicated, may hold values from 512 to 1024
- block_cols: int32 [2], replicated, may hold values from 512 to 1024
- left_ops: bfloat16 [8, 1024, 1024], P('terms', 'rows'), may hold values from -0.1875 to 0.1875
- right_ops: bfloat16 [8, 1024, 1024], P('terms', 'cols'), may hold values from -0.1875 to 0.1875
- source: int32 [8], P('terms'), may hold values from 0 to 1
- target: int32 [8], P('terms'), may hold values from 0 to 1
Outputs:
- sigma: bfloat16 [2, 1024, 1024], P(None, 'rows', 'cols')
- residual: bfloat16 [2, 1024, 1024], P(None, 'rows', 'cols')
Inputs may be any that keep to these rules, and one draw needn't show every extreme that they name: source[t] is the sector whose block term t reads. target[t] is the sector to which term t adds. `block_rows`: entries of a sector block beyond its live left or right states are ignored.
All inputs are finite; a program needn't handle non-finite values.
Results may differ from a plain program's by a relative error of at most 0.0044.
The roundings to bfloat16 on the way count: a program that leaves them out, or rounds other values in their place, can miss the bound.
Values may be sent and summed in bfloat16 or wider, within the bound.
No kernel may reach another device: no remote copies, remote signals or barrier semaphores. Data moves between devices by JAX's collectives and lax.ppermute only.
A program may use at most 64 MiB of HBM per device.

v0:
```python
import jax
import jax.numpy as jnp
from jax import lax
from jax.sharding import PartitionSpec as P

EPSILON = 1e-06


def per_device(wavefunction, energy, block_rows, block_cols, left_ops, right_ops, source, target):
    sectors, tile_rows, tile_cols = wavefunction.shape
    term_count = left_ops.shape[0]
    row_ids = lax.axis_index("rows") * tile_rows + lax.iota(jnp.int32, tile_rows)
    col_ids = lax.axis_index("cols") * tile_cols + lax.iota(jnp.int32, tile_cols)
    inside = (row_ids[None, :, None] < block_rows[:, None, None]) & (
        col_ids[None, None, :] < block_cols[:, None, None]
    )
    live_psi = jnp.where(inside, wavefunction, jnp.zeros_like(wavefunction))
    sector_ids = lax.iota(jnp.int32, sectors)
    partial_value = jnp.zeros((sectors, tile_rows, tile_cols), jnp.float32)
    panels = lax.all_gather(live_psi, "rows", axis=1, tiled=True)
    product_list = []
    for term_index in range(term_count):
        col_panel = lax.dynamic_index_in_dim(panels, source[term_index], 0, keepdims=False)
        product_list.append(
            jnp.dot(left_ops[term_index], col_panel, preferred_element_type=jnp.float32).astype(
                jnp.bfloat16
            )
        )
    products = jnp.stack(product_list)
    additions = jnp.einsum(
        "txl,tml->txm",
        lax.all_gather(products, "cols", axis=2, tiled=True),
        right_ops,
        preferred_element_type=jnp.float32,
    )
    for term_index in range(term_count):
        hit = (sector_ids == target[term_index])[:, None, None]
        partial_value = partial_value + jnp.where(hit, additions[term_index][None], 0.0)
    live_f = live_psi.astype(jnp.float32)
    summed = lax.psum(partial_value, "terms")
    full_sigma = jnp.where(inside, summed + energy[:, None, None] * live_f, 0.0)
    numerator, denominator = lax.psum(
        (jnp.sum(live_f * full_sigma), jnp.sum(live_f * live_f)), ("rows", "cols")
    )
    rayleigh = numerator / (denominator + EPSILON)
    residual = full_sigma - rayleigh * live_f
    return (full_sigma.astype(jnp.bfloat16), residual.astype(jnp.bfloat16))


def solution(mesh):
    in_specs = (
        P(None, "rows", "cols"),
        P(),
        P(),
        P(),
        P("terms", "rows", None),
        P("terms", "cols", None),
        P("terms"),
        P("terms"),
    )
    out_specs = (P(None, "rows", "cols"), P(None, "rows", "cols"))
    return jax.shard_map(
        per_device, mesh=mesh, in_specs=in_specs, out_specs=out_specs, check_vma=False
    )
```

profile of v0, /device:TPU:0, one launch (start us, length us, event | category | flops | bytes accessed | tf_op | source)
XLA Modules:
  0.0 158.2 jit_solution(4470335550946866538)
XLA Ops:
  7.2 0.0 copy-start
  7.2 0.0 all-gather.3.cloned.1.call-start
  7.3 0.9 broadcast_compare_fusion
  8.1 1.8 %and_select_fusion.1 = bf16[2,256,256]{2,1,0:T(8,128)(2,1)} fusion(bf16[2,256,256]{2,1,0:T(8,128)(2,1)} %param.8, pred[2,256]{1,0:T(4,128)(4,1)S(1)} %get-tuple-element.20, pred[2,256]{1,0:T(4,128)(4,1)S(1)} %get-tuple-element.21), kind=kLoop, calls=%fused_computation.13 | loop fusion | flops 262144 | bytes 525312 | tf_op jit(solution)/shard_map/jit(_where)/select_n | solution.py:17
  9.9 0.0 all-gather.3.cloned.1.call-update
  10.0 0.0 all-gather.5.cloned.1.call-start
  10.0 1.5 fusion.31
  19.3 10.4 %all-gather.3.cloned.1.call-done = bf16[2,1024,256]{2,1,0:T(8,128)(2,1)} async-done(((bf16[2,256,256]{2,1,0:T(8,128)(2,1)}), bf16[2,1024,256]{2,1,0:T(8,128)(2,1)}) %all-gather.3.cloned.1.call-update) | async-done | bytes 1048592 | tf_op jit(solution)/shard_map/all_gather | solution.py:20
  29.6 0.0 copy-start.4
  29.6 0.0 copy-start.5
  29.6 1.7 %fusion = bf16[1,256,256]{1,2,0:T(8,128)(2,1)S(1)} fusion(bf16[4,256,1024]{2,1,0:T(8,128)(2,1)} %param.12, bf16[2,1024,256]{2,1,0:T(8,128)(2,1)} %all-gather.3.cloned.1.call-done, s32[]{:T(128)S(6)} %select_n.35), kind=kOutput, calls=%fused_computation.4 | convolution fusion | flops 134283264 | bytes 1179652 | tf_op jit(solution)/shard_map/dot_general | solution.py:25
  31.3 1.6 fusion.1
  32.9 0.0 copy-done.4
  32.9 0.0 copy-start.2
  32.9 1.4 fusion.2
  34.3 0.0 copy-done.5
  34.3 0.4 fusion.3
  34.7 0.9 pad_maximum_fusion
  35.6 0.0 all-gather.5.cloned.1.call-update
  35.6 0.0 all-reduce.3.cloned.1.call-start
  35.6 0.0 copy-done.2
  35.7 0.6 fusion.30
  36.2 1.1 iota_compare_fusion
  37.4 1.3 iota_compare_fusion.2
  38.7 42.7 %all-gather.5.cloned.1.call-done = bf16[4,256,1024]{1,2,0:T(8,128)(2,1)} async-done(((bf16[4,256,256]{1,2,0:T(8,128)(2,1)}), bf16[4,256,1024]{1,2,0:T(8,128)(2,1)}) %all-gather.5.cloned.1.call-update) | async-done | bytes 2097168 | tf_op jit(solution)/shard_map/all_gather | solution.py:32
  81.4 0.0 copy-done
  81.4 2.4 %fusion.32 = f32[4,256,256]{2,1,0:T(8,128)S(1)} fusion(bf16[4,256,1024]{1,2,0:T(8,128)(2,1)} %all-gather.5.cloned.1.call-done, bf16[4,256,1024]{2,1,0:T(8,128)(2,1)S(1)} %copy-done), kind=kOutput, calls=%fused_computation.56 | convolution fusion | flops 536870912 | bytes 5242880 | tf_op jit(solution)/shard_map/txl,tml->txm/dot_general | solution.py:30
  83.9 0.0 copy-start.1
  83.9 0.0 copy-start.3
  83.9 0.1 slice_bitcast_fusion.3
  84.0 1.0 select_add_fusion
  85.0 0.0 all-reduce.3.cloned.1.call-update
  85.0 27.6 %all-reduce.3.cloned.1.call-done = f32[2,256,256]{2,1,0:T(8,128)} async-done(((f32[2,256,256]{2,1,0:T(8,128)}), f32[2,256,256]{2,1,0:T(8,128)}) %all-reduce.3.cloned.1.call-update) | async-done | bytes 524304 | tf_op jit(solution)/shard_map/psum | solution.py:40
  112.6 0.0 copy-done.1
  112.6 0.0 copy-done.3
  112.6 2.0 %fusion.6 = (f32[]{:T(128)}, f32[]{:T(128)}) fusion(f32[2,256,256]{2,1,0:T(8,128)} %all-reduce.3.cloned.1.call-done, f32[2]{0:T(128)S(1)} %copy-done.3, pred[2,256]{1,0:T(4,128)(4,1)S(1)} %get-tuple-element.20, pred[2,256]{1,0:T(4,128)(4,1)S(1)} %get-tuple-element.21, bf16[2,256,256]{2,1,0:T(8,128)(2,1)S(1)} %copy-done.1), kind=kLoop, calls=%fused_computation.16 | loop fusion | flops 1310718 | bytes 787472 | tf_op jit(solution)/shard_map/reduce_sum | solution.py:43
  114.6 33.8 %all-reduce = (f32[]{:T(128)}, f32[]{:T(128)}) all-reduce(f32[]{:T(128)} %get-tuple-element.3, f32[]{:T(128)} %get-tuple-element.2), channel_id=1, replica_groups=mesh['terms'=2,'rows'=4,'cols'=4] {'rows','cols'}, use_global_device_ids=true, to_apply=%region_2.3 | all-reduce | flops 2 | bytes 16 | tf_op jit(solution)/shard_map/psum | solution.py:42
  149.6 2.1 %fusion.8 = (bf16[2,256,256]{2,1,0:T(8,128)(2,1)}, bf16[2,256,256]{2,1,0:T(8,128)(2,1)}) fusion(f32[]{:T(128)S(6)} %div.3, f32[2,256,256]{2,1,0:T(8,128)} %all-reduce.3.cloned.1.call-done, f32[2]{0:T(128)S(1)} %copy-done.3, pred[2,256]{1,0:T(4,128)(4,1)S(1)} %get-tuple-element.20, pred[2,256]{1,0:T(4,128)(4,1)S(1)} %get-tuple-element.21, ...), kind=kLoop, calls=%fused_computation.18 | loop fusion | flops 1310720 | bytes 1311756 | tf_op jit(solution)/shard_map/convert_element_type | solution.py:47
  (2 shorter events, 0.0 us)
Async XLA Ops:
  7.2 74.2 %copy-start = (bf16[4,256,1024]{2,1,0:T(8,128)(2,1)S(1)}, bf16[4,256,1024]{2,1,0:T(8,128)(2,1)}, u32[]{:S(2)}) copy-start(bf16[4,256,1024]{2,1,0:T(8,128)(2,1)} %param.13) | copy-start | bytes 6291460
  7.2 22.4 %all-gather.3.cloned.1.call-start = ((), (), s32[]{:S(2)}) async-start(), calls=%async_computation | async-start | bytes 1310720 | tf_op jit(solution)/shard_map/all_gather | solution.py:20
  10.0 71.4 %all-gather.5.cloned.1.call-start = ((), (), s32[]{:S(2)}) async-start(), calls=%async_computation.1 | async-start | bytes 2621440 | tf_op jit(solution)/shard_map/all_gather | solution.py:32
  29.6 3.3 %copy-start.4 = (bf16[4,256,1024]{2,1,0:T(8,128)(2,1)S(1)}, bf16[4,256,1024]{2,1,0:T(8,128)(2,1)}, u32[]{:S(2)}) copy-start(bf16[4,256,1024]{2,1,0:T(8,128)(2,1)} %param.12) | copy-start | bytes 6291460
  29.6 4.7 %copy-start.5 = (bf16[2,1024,256]{2,1,0:T(8,128)(2,1)S(1)}, bf16[2,1024,256]{2,1,0:T(8,128)(2,1)}, u32[]{:S(2)}) copy-start(bf16[2,1024,256]{2,1,0:T(8,128)(2,1)} %all-gather.3.cloned.1.call-done) | copy-start | bytes 3145732
  32.9 2.7 %copy-start.2 = (s32[4]{0:T(128)S(1)}, s32[4]{0:T(128)}, u32[]{:S(2)}) copy-start(s32[4]{0:T(128)} %param.15) | copy-start | bytes 52
  35.6 77.0 %all-reduce.3.cloned.1.call-start = ((), (), s32[]{:S(2)}) async-start(), calls=%async_computation.2 | async-start | bytes 1048576 | tf_op jit(solution)/shard_map/psum | solution.py:40
  83.9 28.7 %copy-start.1 = (bf16[2,256,256]{2,1,0:T(8,128)(2,1)S(1)}, bf16[2,256,256]{2,1,0:T(8,128)(2,1)}, u32[]{:S(2)}) copy-start(bf16[2,256,256]{2,1,0:T(8,128)(2,1)} %param.8) | copy-start | bytes 786436
  83.9 28.7 %copy-start.3 = (f32[2]{0:T(128)S(1)}, f32[2]{0:T(128)}, u32[]{:S(2)}) copy-start(f32[2]{0:T(128)} %param.9) | copy-start | bytes 28
Sparse Core Ops, SparseCore 0:
  10.1 19.4 all-gather.2
  35.7 45.6 all-gather.4
  85.1 27.4 all-reduce.2
where the time goes:
time: 159 us; the launch traced here: 158 us
  waiting for transfers between devices  80.8 us (51%)
  blocking collectives  33.8 us (21%)
  between operations  23 us (14%)
  other arithmetic  11 us (7%)
  matrix products  7.45 us (5%)
  local copies, waits for them, and re-layouts  2.17 us (1%)
    all_gather x1, waiting for transfers between devices, per_device(): lax.all_gather(products, 'cols', axis=2, tiled=True)  42.7 us
    psum x1, blocking collectives, per_device(): lax.psum((jnp.sum(live_f * full_sigma), jnp.sum(live_f * live_f)), ('rows...  33.8 us
    psum x1, waiting for transfers between devices, per_device(): summed = lax.psum(partial_value, 'terms')  27.6 us
    all_gather x1, waiting for transfers between devices, per_device(): panels = lax.all_gather(live_psi, 'rows', axis=1, tiled=True)  10.4 us
    dot_general x4, matrix products, per_device(): jnp.dot(left_ops[term_index], col_panel, preferred_element_type=jnp.float32)  5 us
  transfers between devices with their start and end apart: 3, of which 3 were waited for; matrix products, arithmetic and copies ran while one was open for 3% of the time, Pallas kernels for 0%

commit v1 on v0

--- a/solution.py
+++ b/solution.py
@@ -40,7 +40,7 @@
     summed = lax.psum(partial_value, "terms")
     full_sigma = jnp.where(inside, summed + energy[:, None, None] * live_f, 0.0)
     numerator, denominator = lax.psum(
-        (jnp.sum(live_f * full_sigma), jnp.sum(live_f * live_f)), ("rows", "cols")
+        lax.psum((jnp.sum(live_f * full_sigma), jnp.sum(live_f * live_f)), "cols"), "rows"
     )
     rayleigh = numerator / (denominator + EPSILON)
     residual = full_sigma - rayleigh * live_f

time: 159 us -> 144 us (0.906)
  blocking collectives: 33.8 us -> 18.6 us
    psum x1 -> x2, blocking collectives: 33.8 us -> 18.6 us  [the longest x1 12.3 us: per_device(): lax.psum((jnp.sum(live_f * full_sigma), jnp.sum(live_f * live_f)), 'cols')]
where the time goes in v1:
time: 144 us; the launch traced here: 143 us
  waiting for transfers between devices  80.8 us (56%)
  between operations  22.8 us (16%)
  blocking collectives  18.6 us (13%)
  other arithmetic  11.1 us (8%)
  matrix products  7.45 us (5%)
  local copies, waits for them, and re-layouts  2.2 us (2%)
    all_gather x1, waiting for transfers between devices, per_device(): lax.all_gather(products, 'cols', axis=2, tiled=True)  42.6 us
    psum x1, waiting for transfers between devices, per_device(): summed = lax.psum(partial_value, 'terms')  27.6 us
    psum x1, blocking collectives, per_device(): lax.psum((jnp.sum(live_f * full_sigma), jnp.sum(live_f * live_f)), 'cols')  12.3 us
    all_gather x1, waiting for transfers between devices, per_device(): panels = lax.all_gather(live_psi, 'rows', axis=1, tiled=True)  10.5 us
    psum x1, blocking collectives, per_device(): lax.psum(lax.psum((jnp.sum(live_f * full_sigma), jnp.sum(live_f * live_f)...  6.27 us
    dot_general x4, matrix products, per_device(): jnp.dot(left_ops[term_index], col_panel, preferred_element_type=jnp.float32)  5 us
  transfers between devices with their start and end apart: 3, of which 3 were waited for; matrix products, arithmetic and copies ran while one was open for 3% of the time, Pallas kernels for 0%

profile of v1, /device:TPU:0, one launch (start us, length us, event | category | flops | bytes accessed | tf_op | source)
XLA Modules:
  0.0 143.0 jit_solution(12156974984244579085)
XLA Ops:
  7.2 0.0 copy-start
  7.2 0.0 all-gather.3.cloned.1.call-start
  7.3 0.9 broadcast_compare_fusion
  8.1 1.8 %and_select_fusion.1 = bf16[2,256,256]{2,1,0:T(8,128)(2,1)} fusion(bf16[2,256,256]{2,1,0:T(8,128)(2,1)} %param.8, pred[2,256]{1,0:T(4,128)(4,1)S(1)} %get-tuple-element.22, pred[2,256]{1,0:T(4,128)(4,1)S(1)} %get-tuple-element.23), kind=kLoop, calls=%fused_computation.13 | loop fusion | flops 262144 | bytes 525312 | tf_op jit(solution)/shard_map/jit(_where)/select_n | solution.py:17
  9.9 0.0 all-gather.3.cloned.1.call-update
  10.0 0.0 all-gather.5.cloned.1.call-start
  10.0 1.5 %fusion.31 = (s32[1]{0:T(128)}, s32[1]{0:T(128)}, s32[1]{0:T(128)}, s32[1]{0:T(128)}) fusion(s32[4]{0:T(128)} %param.14), kind=kLoop, calls=%fused_computation.55 | loop fusion | bytes 32 | tf_op jit(solution)/shard_map/slice | solution.py:23
  19.1 10.5 %all-gather.3.cloned.1.call-done = bf16[2,1024,256]{2,1,0:T(8,128)(2,1)} async-done(((bf16[2,256,256]{2,1,0:T(8,128)(2,1)}), bf16[2,1024,256]{2,1,0:T(8,128)(2,1)}) %all-gather.3.cloned.1.call-update) | async-done | bytes 1048592 | tf_op jit(solution)/shard_map/all_gather | solution.py:20
  29.6 0.0 copy-start.4
  29.6 0.0 copy-start.5
  29.6 1.7 %fusion = bf16[1,256,256]{1,2,0:T(8,128)(2,1)S(1)} fusion(bf16[4,256,1024]{2,1,0:T(8,128)(2,1)} %param.12, bf16[2,1024,256]{2,1,0:T(8,128)(2,1)} %all-gather.3.cloned.1.call-done, s32[]{:T(128)S(6)} %select_n.35), kind=kOutput, calls=%fused_computation.4 | convolution fusion | flops 134283264 | bytes 1179652 | tf_op jit(solution)/shard_map/dot_general | solution.py:25
  31.3 1.6 %fusion.1 = bf16[1,256,256]{1,2,0:T(8,128)(2,1)S(1)} fusion(bf16[4,256,1024]{2,1,0:T(8,128)(2,1)} %param.12, bf16[2,1024,256]{2,1,0:T(8,128)(2,1)} %all-gather.3.cloned.1.call-done, s32[]{:T(128)S(6)} %select_n.36), kind=kOutput, calls=%fused_computation.5 | convolution fusion | flops 134283264 | bytes 1179652 | tf_op jit(solution)/shard_map/dot_general | solution.py:25
  32.9 0.0 copy-done.4
  32.9 0.0 copy-start.2
  32.9 1.4 fusion.2
  34.3 0.0 copy-done.5
  34.3 0.4 fusion.3
  34.7 0.9 pad_maximum_fusion
  35.6 0.0 all-gather.5.cloned.1.call-update
  35.6 0.0 all-reduce.4.cloned.1.call-start
  35.6 0.0 copy-done.2
  35.6 0.6 fusion.30
  36.3 1.2 iota_compare_fusion
  37.5 1.3 iota_compare_fusion.2
  38.8 42.6 %all-gather.5.cloned.1.call-done = bf16[4,256,1024]{1,2,0:T(8,128)(2,1)} async-done(((bf16[4,256,256]{1,2,0:T(8,128)(2,1)}), bf16[4,256,1024]{1,2,0:T(8,128)(2,1)}) %all-gather.5.cloned.1.call-update) | async-done | bytes 2097168 | tf_op jit(solution)/shard_map/all_gather | solution.py:32
  81.4 0.0 copy-done
  81.4 2.4 %fusion.32 = f32[4,256,256]{2,1,0:T(8,128)S(1)} fusion(bf16[4,256,1024]{1,2,0:T(8,128)(2,1)} %all-gather.5.cloned.1.call-done, bf16[4,256,1024]{2,1,0:T(8,128)(2,1)S(1)} %copy-done), kind=kOutput, calls=%fused_computation.56 | convolution fusion | flops 536870912 | bytes 5242880 | tf_op jit(solution)/shard_map/txl,tml->txm/dot_general | solution.py:30
  83.9 0.0 copy-start.1
  83.9 0.0 copy-start.3
  83.9 0.1 slice_bitcast_fusion.3
  84.0 1.0 select_add_fusion
  84.9 0.0 all-reduce.4.cloned.1.call-update
  85.0 27.6 %all-reduce.4.cloned.1.call-done = f32[2,256,256]{2,1,0:T(8,128)} async-done(((f32[2,256,256]{2,1,0:T(8,128)}), f32[2,256,256]{2,1,0:T(8,128)}) %all-reduce.4.cloned.1.call-update) | async-done | bytes 524304 | tf_op jit(solution)/shard_map/psum | solution.py:40
  112.6 0.0 copy-done.1
  112.6 0.0 copy-done.3
  112.6 2.0 %fusion.6 = (f32[]{:T(128)}, f32[]{:T(128)}) fusion(f32[2,256,256]{2,1,0:T(8,128)} %all-reduce.4.cloned.1.call-done, f32[2]{0:T(128)S(1)} %copy-done.3, pred[2,256]{1,0:T(4,128)(4,1)S(1)} %get-tuple-element.22, pred[2,256]{1,0:T(4,128)(4,1)S(1)} %get-tuple-element.23, bf16[2,256,256]{2,1,0:T(8,128)(2,1)S(1)} %copy-done.1), kind=kLoop, calls=%fused_computation.16 | loop fusion | flops 1310718 | bytes 787472 | tf_op jit(solution)/shard_map/reduce_sum | solution.py:43
  114.5 12.3 %all-reduce = (f32[]{:T(128)}, f32[]{:T(128)}) all-reduce(f32[]{:T(128)} %get-tuple-element.3, f32[]{:T(128)} %get-tuple-element.2), channel_id=1, replica_groups=mesh['terms'=2,'rows'=4,'cols'=4] {'cols'}, use_global_device_ids=true, to_apply=%region_2.3 | all-reduce | flops 2 | bytes 16 | tf_op jit(solution)/shard_map/psum | solution.py:43
  126.8 6.3 %all-reduce.1 = (f32[]{:T(128)}, f32[]{:T(128)}) all-reduce(f32[]{:T(128)} %get-tuple-element.4, f32[]{:T(128)} %get-tuple-element.5), channel_id=1, replica_groups=mesh['terms'=2,'rows'=4,'cols'=4] {'rows'}, use_global_device_ids=true, to_apply=%region_3.4 | all-reduce | flops 2 | bytes 16 | tf_op jit(solution)/shard_map/psum | solution.py:42
  134.4 2.1 %fusion.8 = (bf16[2,256,256]{2,1,0:T(8,128)(2,1)}, bf16[2,256,256]{2,1,0:T(8,128)(2,1)}) fusion(f32[]{:T(128)S(6)} %div.3, f32[2,256,256]{2,1,0:T(8,128)} %all-reduce.4.cloned.1.call-done, f32[2]{0:T(128)S(1)} %copy-done.3, pred[2,256]{1,0:T(4,128)(4,1)S(1)} %get-tuple-element.22, pred[2,256]{1,0:T(4,128)(4,1)S(1)} %get-tuple-element.23, ...), kind=kLoop, calls=%fused_computation.18 | loop fusion | flops 1310720 | bytes 1311756 | tf_op jit(solution)/shard_map/convert_element_type | solution.py:47
  (2 shorter events, 0.0 us)
Async XLA Ops:
  7.2 74.2 %copy-start = (bf16[4,256,1024]{2,1,0:T(8,128)(2,1)S(1)}, bf16[4,256,1024]{2,1,0:T(8,128)(2,1)}, u32[]{:S(2)}) copy-start(bf16[4,256,1024]{2,1,0:T(8,128)(2,1)} %param.13) | copy-start | bytes 6291460
  7.2 22.4 %all-gather.3.cloned.1.call-start = ((), (), s32[]{:S(2)}) async-start(), calls=%async_computation | async-start | bytes 1310720 | tf_op jit(solution)/shard_map/all_gather | solution.py:20
  10.0 71.4 %all-gather.5.cloned.1.call-start = ((), (), s32[]{:S(2)}) async-start(), calls=%async_computation.1 | async-start | bytes 2621440 | tf_op jit(solution)/shard_map/all_gather | solution.py:32
  29.6 3.3 %copy-start.4 = (bf16[4,256,1024]{2,1,0:T(8,128)(2,1)S(1)}, bf16[4,256,1024]{2,1,0:T(8,128)(2,1)}, u32[]{:S(2)}) copy-start(bf16[4,256,1024]{2,1,0:T(8,128)(2,1)} %param.12) | copy-start | bytes 6291460
  29.6 4.7 %copy-start.5 = (bf16[2,1024,256]{2,1,0:T(8,128)(2,1)S(1)}, bf16[2,1024,256]{2,1,0:T(8,128)(2,1)}, u32[]{:S(2)}) copy-start(bf16[2,1024,256]{2,1,0:T(8,128)(2,1)} %all-gather.3.cloned.1.call-done) | copy-start | bytes 3145732
  32.9 2.7 %copy-start.2 = (s32[4]{0:T(128)S(1)}, s32[4]{0:T(128)}, u32[]{:S(2)}) copy-start(s32[4]{0:T(128)} %param.15) | copy-start | bytes 52
  35.6 77.0 %all-reduce.4.cloned.1.call-start = ((), (), s32[]{:S(2)}) async-start(), calls=%async_computation.2 | async-start | bytes 1048576 | tf_op jit(solution)/shard_map/psum | solution.py:40
  83.9 28.7 %copy-start.1 = (bf16[2,256,256]{2,1,0:T(8,128)(2,1)S(1)}, bf16[2,256,256]{2,1,0:T(8,128)(2,1)}, u32[]{:S(2)}) copy-start(bf16[2,256,256]{2,1,0:T(8,128)(2,1)} %param.8) | copy-start | bytes 786436
  83.9 28.7 %copy-start.3 = (f32[2]{0:T(128)S(1)}, f32[2]{0:T(128)}, u32[]{:S(2)}) copy-start(f32[2]{0:T(128)} %param.9) | copy-start | bytes 28
Sparse Core Ops, SparseCore 0:
  10.1 19.4 all-gather.2
  35.7 45.6 all-gather.4
  85.1 27.4 all-reduce.3
